TPU v7x, 256 devices: a whole 4x4x8 slice. The times are simulated.
256 devices in a mesh: dp: 8 (over x, core), cls: 32 (over z, y).
Axes of the slice: x: 4, y: 4, z: 8, core: 2. Of those that a mesh axis runs over, the one named last changes fastest.
Arguments:
- centers: float32 [65536, 512], P('cls'), may hold values from -6 to 6
- momentum: float32 [65536, 512], P('cls'), may hold values from -6 to 6
- grad_rows: bfloat16 [1048576, 512], P(('dp', 'cls')), may hold values from -5400 to 5400
- row_ids: int32 [1048576], P(('dp', 'cls')), may hold values from -1 to 65535, as said below
Outputs:
- new_centers: float32 [65536, 512], P('cls')
- new_momentum: float32 [65536, 512], P('cls')
Inputs may be any that keep to these rules, and one draw needn't show every extreme that they name: `row_ids`: slots of one device come in 32 blocks of 128; block o holds only rows o * 2048 to (o + 1) * 2048 - 1 or -1; within a block the used slots come first, distinct and ascending, and one to 128 of them are used. In every draw, for some owner o, every device of some index of dp fills its whole block o.
All inputs are finite; a program needn't handle non-finite values.
Results may differ from a plain program's by a relative error of at most 0.0003.
Values may be sent and summed in bfloat16 or wider, within the bound.
A program may use at most 128 MiB of HBM per device.

v0:
```python
import math
import jax
import jax.numpy as jnp
from jax import lax
from jax.sharding import PartitionSpec as P

beta_decay = 0.9
learn_rate = 0.5
clip_rms = 1.0
eps_norm = 1e-06
eps_row = 1e-06


def padded_to(lines, peers):
    spare = -lines.shape[0] % peers
    if not spare:
        return lines
    return jnp.concatenate([lines, jnp.zeros((spare, *lines.shape[1:]), lines.dtype)])


def sum_by_parts(array, axis):
    lines = array.reshape(-1, *array.shape[1:][-1:])
    padded = padded_to(lines, lax.axis_size(axis))
    own = lax.psum_scatter(padded, axis, scatter_dimension=0, tiled=True)
    whole = lax.all_gather(own, axis, axis=0, tiled=True)
    return whole[: len(lines)].reshape(array.shape)


def from_everyone(array, axis):
    peers = lax.axis_size(axis)
    return lax.all_to_all(
        jnp.broadcast_to(array[None], (peers, *array.shape)), axis, 0, 0, tiled=True
    )


def of_everyone(array, axis):
    return from_everyone(array, axis).sum(axis=0)


def on_device(centers, momentum, grad_rows, row_ids):
    groups = lax.axis_size("cls")
    rows_dev = centers.shape[0]
    features = centers.shape[1]
    capacity = grad_rows.shape[0] // groups
    owner_of = lax.broadcasted_iota(jnp.int32, (groups, capacity), 0)
    sent_ids = row_ids.reshape(groups, capacity)
    local_ids = jnp.where(sent_ids >= 0, sent_ids - owner_of * rows_dev, -1)
    blocks = grad_rows.reshape(groups, capacity, features)
    got_rows, got_ids = (
        lax.all_to_all(blocks, "cls", split_axis=0, concat_axis=0, tiled=True),
        lax.all_to_all(local_ids, "cls", split_axis=0, concat_axis=0, tiled=True),
    )
    flat_rows = got_rows.reshape(groups * capacity, features)
    flat_ids = got_ids.reshape(groups * capacity)
    decayed = beta_decay * momentum
    onehot_rows = lax.broadcasted_iota(jnp.int32, (rows_dev, flat_ids.shape[0]), 0)
    table = (onehot_rows == flat_ids[None, :]).astype(jnp.bfloat16)
    partial_value = jnp.dot(table, flat_rows, preferred_element_type=jnp.float32)
    gradient = sum_by_parts(partial_value, "dp")
    squares = of_everyone(jnp.sum(gradient * gradient), "cls")
    ceiling = clip_rms * math.sqrt(rows_dev * groups * features)
    factor = jnp.minimum(1.0, ceiling / jnp.sqrt(squares + eps_norm))
    new_momentum = decayed + factor * gradient
    stepped = centers - learn_rate * new_momentum
    rescale = lax.rsqrt(jnp.mean(stepped * stepped, axis=1, keepdims=True) + eps_row)
    return (stepped * rescale, new_momentum)


def solution(mesh):
    placed = (P("cls", None), P("cls", None), P(("dp", "cls"), None), P(("dp", "cls")))
    return jax.shard_map(
        on_device,
        mesh=mesh,
        in_specs=placed,
        out_specs=(P("cls", None), P("cls", None)),
        check_vma=False,
    )
```

profile of v0, /device:TPU:1, one launch (start us, length us, event | category | flops | bytes accessed | tf_op | source)
XLA Modules:
  0.0 251.9 jit_solution(12827942257511966301)
XLA Ops:
  7.2 0.0 reduce-scatter.2.cloned.1.call-start
  7.2 0.8 compare_select_fusion
  8.0 20.4 %all_to_all.17 = s32[32,1,128]{2,1,0:T(1,128)S(1)} all-to-all(s32[32,1,128]{2,1,0:T(1,128)S(1)} %compare_select_fusion), channel_id=1, replica_groups=mesh['dp'=8,'cls'=32] {'cls'}, dimensions={0} | all-to-all | bytes 32768 | tf_op jit(solution)/shard_map/all_to_all | solution.py:51
  28.5 96.8 %all_to_all.18 = bf16[32,128,512]{2,1,0:T(8,128)(2,1)S(1)} all-to-all(bf16[32,128,512]{2,1,0:T(8,128)(2,1)} %bitcast.5), channel_id=1, replica_groups=mesh['dp'=8,'cls'=32] {'cls'}, dimensions={0} | all-to-all | bytes 8388608 | tf_op jit(solution)/shard_map/all_to_all | solution.py:50
  125.3 10.3 %fusion = f32[2048,512]{1,0:T(8,128)} fusion(bf16[4096,512]{1,0:T(8,128)(2,1)S(1)} %bitcast.6, s32[4096]{0:T(1024)S(1)} %bitcast.8), kind=kOutput, calls=%fused_computation.1 | convolution fusion | flops 8598323200 | bytes 8404992 | tf_op jit(solution)/shard_map/dot_general | solution.py:58
  135.6 0.0 reduce-scatter.2.cloned.1.call-update
  135.6 0.0 all-gather.2.cloned.1.call-start
  135.7 37.9 %reduce-scatter.2.cloned.1.call-done = f32[256,512]{1,0:T(8,128)} async-done(((f32[2048,512]{1,0:T(8,128)}), f32[256,512]{1,0:T(8,128)}) %reduce-scatter.2.cloned.1.call-update) | async-done | bytes 524304 | tf_op jit(solution)/shard_map/reduce_scatter | solution.py:24
  173.5 0.0 all-gather.2.cloned.1.call-update
  173.6 38.6 %all-gather.2.cloned.1.call-done = f32[2048,512]{1,0:T(8,128)} async-done(((f32[256,512]{1,0:T(8,128)}), f32[2048,512]{1,0:T(8,128)}) %all-gather.2.cloned.1.call-update) | async-done | bytes 4194320 | tf_op jit(solution)/shard_map/all_gather | solution.py:25
  212.1 3.9 %multiply_reduce_fusion.1 = f32[]{:T(128)} fusion(f32[2048,512]{1,0:T(8,128)} %all-gather.2.cloned.1.call-done), kind=kLoop, calls=%fused_computation.6 | loop fusion | flops 2097151 | bytes 4194308 | tf_op jit(solution)/shard_map/reduce_sum | solution.py:60
  216.0 0.7 broadcast_in_dim.12
  216.7 18.0 %all_to_all.19 = f32[32,1,1]{2,1,0:T(1,128)S(1)} all-to-all(f32[32,1,1]{2,1,0:T(1,128)S(1)} %broadcast_in_dim.12), channel_id=1, replica_groups=mesh['dp'=8,'cls'=32] {'cls'}, dimensions={0} | all-to-all | bytes 256 | tf_op jit(solution)/shard_map/all_to_all | solution.py:31
  234.7 0.6 reduce_sum.28
  236.0 0.0 copy-start
  236.0 5.8 %multiply_reduce_fusion = (f32[2048]{0:T(1024)S(1)}, f32[2048,512]{1,0:T(8,128)S(1)}) fusion(f32[2048,512]{1,0:T(8,128)} %param.4, f32[2048,512]{1,0:T(8,128)} %all-gather.2.cloned.1.call-done, f32[]{:T(128)S(6)} %min_shard_map.3, f32[2048,512]{1,0:T(8,128)} %param.5), kind=kLoop, calls=%fused_computation.3 | loop fusion | flops 7337984 | bytes 16785412 | tf_op jit(solution)/shard_map/reduce_sum | solution.py:65
  241.8 0.0 copy-start.1
  241.8 0.0 copy-done
  241.8 2.8 %broadcast_multiply_fusion = f32[2048,512]{1,0:T(8,128)} fusion(f32[2048]{0:T(1024)S(1)} %add_rsqrt_fusion, f32[2048,512]{1,0:T(8,128)S(1)} %copy-done, f32[2048,512]{1,0:T(8,128)S(1)} %get-tuple-element.3), kind=kLoop, calls=%fused_computation.7 | loop fusion | flops 3145728 | bytes 12591104 | tf_op jit(solution)/shard_map/mul | solution.py:66
  244.7 0.4 copy-done.1
  (2 shorter events, 0.0 us)
Async XLA Ops:
  7.2 166.4 %reduce-scatter.2.cloned.1.call-start = ((), (), s32[]{:S(2)}) async-start(), calls=%async_computation.4 | async-start | bytes 4718592 | tf_op jit(solution)/shard_map/reduce_scatter | solution.py:24
  135.6 76.5 %all-gather.2.cloned.1.call-start = ((), (), s32[]{:S(2)}) async-start(), calls=%async_computation.5 | async-start | bytes 4718592 | tf_op jit(solution)/shard_map/all_gather | solution.py:25
  236.0 5.9 %copy-start = (f32[2048,512]{1,0:T(8,128)S(1)}, f32[2048,512]{1,0:T(8,128)}, u32[]{:S(2)}) copy-start(f32[2048,512]{1,0:T(8,128)} %param.4) | copy-start | bytes 12582916
  241.8 3.3 %copy-start.1 = (f32[2048,512]{1,0:T(8,128)}, f32[2048,512]{1,0:T(8,128)S(1)}, u32[]{:S(2)}) copy-start(f32[2048,512]{1,0:T(8,128)S(1)} %get-tuple-element.3) | copy-start | bytes 12582916
Sparse Core Ops, SparseCore 0:
  135.7 37.7 reduce-scatter.1
  175.4 36.6 all-gather.1
where the time goes:
time: 252 us
  blocking collectives  135 us (54%)
  waiting for transfers between devices  76.5 us (30%)
  between operations  14.8 us (6%)
  other arithmetic  14 us (6%)
  matrix products  10.3 us (4%)
    all_to_all x1, blocking collectives, on_device(): lax.all_to_all(blocks, 'cls', split_axis=0, concat_axis=0, tiled=True)  96.8 us
    all_gather x1, waiting for transfers between devices, sum_by_parts(): whole = lax.all_gather(own, axis, axis=0, tiled=True)  38.6 us
    reduce_scatter x1, waiting for transfers between devices, sum_by_parts(): own = lax.psum_scatter(padded, axis, scatter_dimension=0, tiled=True)  37.9 us
    all_to_all x1, blocking collectives, on_device(): lax.all_to_all(local_ids, 'cls', split_axis=0, concat_axis=0, tiled=True)  20.4 us
    all_to_all x1, blocking collectives, from_everyone(): lax.all_to_all(jnp.broadcast_to(array[None], (peers, *array.shape)), axis...  18 us
    dot_general x1, matrix products, on_device(): jnp.dot(table, flat_rows, preferred_element_type=jnp.float32)  10.3 us
    reduce_sum x1, other arithmetic, on_device(): jnp.mean(stepped * stepped, axis=1, keepdims=True) + eps_row  5.82 us
  transfers between devices with their start and end apart: 2, of which 2 were waited for; matrix products, arithmetic and copies ran while one was open for 0% of the time, Pallas kernels for 0%

commit v1 on v0

--- a/solution.py
+++ b/solution.py
@@ -22,7 +22,10 @@
     lines = array.reshape(-1, *array.shape[1:][-1:])
     padded = padded_to(lines, lax.axis_size(axis))
     own = lax.psum_scatter(padded, axis, scatter_dimension=0, tiled=True)
-    whole = lax.all_gather(own, axis, axis=0, tiled=True)
+    peers_2 = lax.axis_size(axis)
+    pieces = jnp.stack([own for _ in range(peers_2)])
+    pieces = lax.all_to_all(pieces, axis, split_axis=0, concat_axis=0)
+    whole = jnp.concatenate(pieces, axis=0)
     return whole[: len(lines)].reshape(array.shape)
 
 

time: 252 us -> 270 us (1.071)
  blocking collectives: 135 us -> 190 us
  waiting for transfers between devices: 76.5 us -> 37.9 us
  local copies, waits for them, and re-layouts: 1.09 us -> 6.52 us
  other arithmetic: 14 us -> 9.69 us
    all_to_all x0 -> x1, blocking collectives: none -> 54.5 us  [sum_by_parts(): pieces = lax.all_to_all(pieces, axis, split_axis=0, concat_axis=0)]
    all_gather x1 -> x0, waiting for transfers between devices: 38.6 us -> none  [sum_by_parts(): whole = lax.all_gather(own, axis, axis=0, tiled=True)]
    reduce_sum x1, other arithmetic: 5.82 us -> 0.89 us  [on_device(): jnp.mean(stepped * stepped, axis=1, keepdims=True) + eps_row]
    unnamed x4 -> x8, local copies, waits for them, and re-layouts: 0.44 us -> 4.3 us
    mul x0 -> x1, other arithmetic: none -> 2.86 us  [on_device(): new_momentum = decayed + factor * gradient]
  transfers between devices with their start and end apart: 2 -> 1, of which waited for: 2 -> 1; matrix products, arithmetic and copies ran while one was open for 0% -> 0% of each run, Pallas kernels for 0% -> 0%
where the time goes in v1:
time: 270 us; the launch traced here: 269 us
  blocking collectives  190 us (70%)
  waiting for transfers between devices  37.9 us (14%)
  between operations  14.8 us (5%)
  matrix products  10.3 us (4%)
  other arithmetic  9.69 us (4%)
  local copies, waits for them, and re-layouts  6.52 us (2%)
    all_to_all x1, blocking collectives, on_device(): lax.all_to_all(blocks, 'cls', split_axis=0, concat_axis=0, tiled=True)  96.8 us
    all_to_all x1, blocking collectives, sum_by_parts(): pieces = lax.all_to_all(pieces, axis, split_axis=0, concat_axis=0)  54.5 us
    reduce_scatter x1, waiting for transfers between devices, sum_by_parts(): own = lax.psum_scatter(padded, axis, scatter_dimension=0, tiled=True)  37.9 us
    all_to_all x1, blocking collectives, on_device(): lax.all_to_all(local_ids, 'cls', split_axis=0, concat_axis=0, tiled=True)  20.4 us
    all_to_all x1, blocking collectives, from_everyone(): lax.all_to_all(jnp.broadcast_to(array[None], (peers, *array.shape)), axis...  18.1 us
    dot_general x1, matrix products, on_device(): jnp.dot(table, flat_rows, preferred_element_type=jnp.float32)  10.3 us
  transfers between devices with their start and end apart: 1, of which 1 were waited for; matrix products, arithmetic and copies ran while one was open for 0% of the time, Pallas kernels for 0%

profile of v1, /device:TPU:1, one launch (start us, length us, event | category | flops | bytes accessed | tf_op | source)
XLA Modules:
  0.0 269.1 jit_solution(4219259355161516408)
XLA Ops:
  7.2 0.0 reduce-scatter.2.cloned.1.call-start
  7.2 0.8 compare_select_fusion
  8.0 20.4 %all_to_all.22 = s32[32,1,128]{2,1,0:T(1,128)S(1)} all-to-all(s32[32,1,128]{2,1,0:T(1,128)S(1)} %compare_select_fusion), channel_id=1, replica_groups=mesh['dp'=8,'cls'=32] {'cls'}, dimensions={0} | all-to-all | bytes 32768 | tf_op jit(solution)/shard_map/all_to_all | solution.py:54
  28.5 96.8 %all_to_all.23 = bf16[32,128,512]{2,1,0:T(8,128)(2,1)S(1)} all-to-all(bf16[32,128,512]{2,1,0:T(8,128)(2,1)} %bitcast.8), channel_id=1, replica_groups=mesh['dp'=8,'cls'=32] {'cls'}, dimensions={0} | all-to-all | bytes 8388608 | tf_op jit(solution)/shard_map/all_to_all | solution.py:53
  125.3 10.3 %fusion = f32[2048,512]{1,0:T(8,128)} fusion(bf16[4096,512]{1,0:T(8,128)(2,1)S(1)} %bitcast.9, s32[4096]{0:T(1024)S(1)} %bitcast.11), kind=kOutput, calls=%fused_computation.1 | convolution fusion | flops 8598323200 | bytes 8404992 | tf_op jit(solution)/shard_map/dot_general | solution.py:61
  135.6 0.0 reduce-scatter.2.cloned.1.call-update
  135.6 37.9 %reduce-scatter.2.cloned.1.call-done = f32[256,512]{1,0:T(8,128)} async-done(((f32[2048,512]{1,0:T(8,128)}), f32[256,512]{1,0:T(8,128)}) %reduce-scatter.2.cloned.1.call-update) | async-done | bytes 524304 | tf_op jit(solution)/shard_map/reduce_scatter | solution.py:24
  173.5 1.6 stack.2
  175.1 54.5 %all_to_all.24 = f32[8,256,512]{2,1,0:T(8,128)S(1)} all-to-all(f32[8,256,512]{2,1,0:T(8,128)S(1)} %stack.2), channel_id=1, replica_groups=mesh['dp'=8,'cls'=32] {'dp'}, dimensions={0} | all-to-all | bytes 8388608 | tf_op jit(solution)/shard_map/all_to_all | solution.py:27
  229.6 0.0 copy-start
  229.6 2.0 copy-done
  231.6 1.7 multiply_reduce_fusion.1
  233.3 0.7 broadcast_in_dim.12
  233.9 18.1 %all_to_all.25 = f32[32,1,1]{2,1,0:T(1,128)S(1)} all-to-all(f32[32,1,1]{2,1,0:T(1,128)S(1)} %broadcast_in_dim.12), channel_id=1, replica_groups=mesh['dp'=8,'cls'=32] {'cls'}, dimensions={0} | all-to-all | bytes 256 | tf_op jit(solution)/shard_map/all_to_all | solution.py:34
  252.0 0.6 reduce_sum.28
  253.4 0.0 copy-start.1
  253.4 0.0 copy-start.3
  253.4 2.9 %broadcast_multiply_fusion.1 = f32[8,256,512]{2,1,0:T(8,128)S(1)} fusion(f32[8,256,512]{2,1,0:T(8,128)} %copy-done, f32[]{:T(128)S(6)} %min_shard_map.3), kind=kLoop, calls=%fused_computation.8 | loop fusion | flops 1048576 | bytes 8388612 | tf_op jit(solution)/shard_map/mul | solution.py:66
  256.2 0.6 copy-done.1
  256.8 1.3 copy-done.3
  258.1 0.9 multiply_reduce_fusion
  259.0 0.0 copy-start.2
  259.0 2.8 %broadcast_multiply_fusion = f32[2048,512]{1,0:T(8,128)} fusion(f32[2048]{0:T(1024)S(1)} %add_rsqrt_fusion, f32[2048,512]{1,0:T(8,128)S(1)} %copy-done.1, f32[2048,512]{1,0:T(8,128)S(1)} %get-tuple-element.3), kind=kLoop, calls=%fused_computation.7 | loop fusion | flops 3145728 | bytes 12591104 | tf_op jit(solution)/shard_map/mul | solution.py:69
  261.8 0.4 copy-done.2
  (2 shorter events, 0.0 us)
Async XLA Ops:
  7.2 166.4 %reduce-scatter.2.cloned.1.call-start = ((), (), s32[]{:S(2)}) async-start(), calls=%async_computation.5 | async-start | bytes 4718592 | tf_op jit(solution)/shard_map/reduce_scatter | solution.py:24
  229.6 2.0 copy-start
  253.4 3.5 %copy-start.1 = (f32[2048,512]{1,0:T(8,128)S(1)}, f32[2048,512]{1,0:T(8,128)}, u32[]{:S(2)}) copy-start(f32[2048,512]{1,0:T(8,128)} %param.4) | copy-start | bytes 12582916
  253.4 4.7 %copy-start.3 = (f32[2048,512]{1,0:T(8,128)S(1)}, f32[2048,512]{1,0:T(8,128)}, u32[]{:S(2)}) copy-start(f32[2048,512]{1,0:T(8,128)} %param.5) | copy-start | bytes 12582916
  259.0 3.3 %copy-start.2 = (f32[2048,512]{1,0:T(8,128)}, f32[2048,512]{1,0:T(8,128)S(1)}, u32[]{:S(2)}) copy-start(f32[2048,512]{1,0:T(8,128)S(1)} %get-tuple-element.3) | copy-start | bytes 12582916
Sparse Core Ops, SparseCore 0:
  135.7 37.7 reduce-scatter.1
